TPU v7x, 32 devices: a whole 2x2x4 slice. The times are simulated.
32 devices in a mesh: band: 16 (over z, y, core), slab: 2 (over x).
Axes of the slice: x: 2, y: 2, z: 4, core: 2. Of those that a mesh axis runs over, the one named last changes fastest.
Arguments:
- orbitals: bfloat16 [32, 32, 4096], P('band', 'slab'), may hold values from -6 to 6
- occupation: bfloat16 [32], P('band'), may hold values from 0.25 to 1
Outputs:
- exchange_field: float32 [32, 32, 4096], P('band', 'slab')
All inputs are finite; a program needn't handle non-finite values.
Results may differ from a plain program's by a relative error of at most 0.001.
Values may be sent and summed in bfloat16 or wider, within the bound.
A program may use at most 64 MiB of HBM per device.

v0:
```python
import math

import jax
import jax.numpy as jnp
from jax import lax
from jax.sharding import PartitionSpec as P

NZ = 64
STEPS = 3


screening = 0.5
ratio_mid = (12.0 + 2.0 * screening) / 12.0
root_term = math.sqrt(ratio_mid * ratio_mid - 1.0)
decay_ratio = ratio_mid - root_term
coeff_zero = 1.0 / (6.0 * root_term)
coeff_one = -2.0 * decay_ratio * coeff_zero
coeff_two = 2.0 * decay_ratio * decay_ratio * coeff_zero


def with_halo(array, sides, width):
    for axis, dim in sides:
        size, length = (lax.axis_size(axis), array.shape[dim])
        up = [(i, (i + 1) % size) for i in range(size - 1)]
        down = [(j, i) for i, j in up]
        last = lax.slice_in_dim(array, length - width, length, axis=dim)
        leading = lax.slice_in_dim(array, 0, width, axis=dim)
        before = lax.ppermute(last, axis, up)
        after = lax.ppermute(leading, axis, down)
        array = jnp.concatenate([before, array, after], axis=dim)
    return array


def passed_along(array, axis, by):
    size = lax.axis_size(axis)
    return lax.ppermute(array, axis, [(i, (i + by) % size) for i in range(size)])


def cross_sum(values):
    rest = ((0, 0),) * (values.ndim - 1)
    padded_y = jnp.pad(values, rest + ((NZ, NZ),))
    along_y = padded_y[..., 2 * NZ :] + padded_y[..., : -2 * NZ]
    narrow = jnp.pad(values, rest + ((1, 1),))
    column = jnp.arange(values.shape[-1], dtype=jnp.int32) % NZ
    left_side = jnp.where(column != 0, narrow[..., :-2], 0.0)
    right_side = jnp.where(column != NZ - 1, narrow[..., 2:], 0.0)
    return along_y + (left_side + right_side)


def neighbour_planes(extended):
    return extended[:, :, 2:] + extended[:, :, :-2] + cross_sum(extended[:, :, 1:-1])


def per_device(orbitals, occupation):
    planes = orbitals.shape[1]
    own_extended = with_halo(orbitals, (("slab", 1),), 2)
    own_wide = own_extended.astype(jnp.float32)
    running = jnp.zeros(orbitals.shape, jnp.float32)
    visiting = (orbitals, occupation)
    for visit in range(STEPS + 1):
        if visit > 0:
            visiting = passed_along((visiting[0], visiting[1]), "band", 1)
        visitor_orbitals, visitor_weights = visiting
        if visit == 0:
            visitor_wide = own_wide
        else:
            visitor_wide = with_halo(visitor_orbitals, (("slab", 1),), 2).astype(jnp.float32)
        density_wide = own_wide[:, None] * visitor_wide[None]
        first_wide = -neighbour_planes(density_wide) / 6.0
        global_plane = lax.axis_index("slab") * planes + jnp.arange(planes + 2, dtype=jnp.int32) - 1
        inside = (global_plane >= 0) & (global_plane < planes * lax.axis_size("slab"))
        first_wide = jnp.where(inside[:, None], first_wide, 0.0)
        density = density_wide[:, :, 2:-2]
        first_term = first_wide[:, :, 1:-1]
        second_term = -neighbour_planes(first_wide) / 3.0 - density
        potential = coeff_zero * density + coeff_one * first_term + coeff_two * second_term
        visitor = visitor_orbitals.astype(jnp.float32)
        weights = visitor_weights.astype(jnp.float32)
        running = running - jnp.sum(
            weights[None, :, None, None] * visitor[None] * potential, axis=1
        )
    return running


def solution(mesh):
    in_specs = (P("band", "slab", None), P("band"))
    out_specs = P("band", "slab", None)
    return jax.shard_map(
        per_device, mesh=mesh, in_specs=in_specs, out_specs=out_specs, check_vma=False
    )
```

profile of v0, /device:TPU:0, one launch (start us, length us, event | category | flops | bytes accessed | tf_op | source)
XLA Modules:
  0.0 96.9 jit_solution(1965996722033846472)
XLA Ops:
  1.5 4.4 %collective-permute-start = (bf16[2,2,4096]{2,1,0:T(2,128)(2,1)S(1)}, bf16[2,2,4096]{2,1,0:T(2,128)(2,1)S(1)}, u32[]{:S(2)}, u32[]{:S(2)}) collective-permute-start(bf16[2,2,4096]{2,1,0:T(2,128)(2,1)S(1)} %get-tuple-element.17), channel_id=1, source_target_pairs={{0,1},{2,3},{4,5},{6,7},{8,9},{10,11},{12,13},{14,15},{16,17},{18,... | collective-permute-start | bytes 98312 | tf_op jit(solution)/shard_map/ppermute | solution.py:28
  5.9 1.3 %collective-permute-start.1 = (bf16[2,2,4096]{2,1,0:T(2,128)(2,1)S(1)}, bf16[2,2,4096]{2,1,0:T(2,128)(2,1)S(1)}, u32[]{:S(2)}, u32[]{:S(2)}) collective-permute-start(bf16[2,2,4096]{2,1,0:T(2,128)(2,1)S(1)} %get-tuple-element.18), channel_id=1, source_target_pairs={{1,0},{3,2},{5,4},{7,6},{9,8},{11,10},{13,12},{15,14},{17,16},{19,... | collective-permute-start | bytes 98312 | tf_op jit(solution)/shard_map/ppermute | solution.py:29
  7.2 1.4 %collective-permute-start.2 = (bf16[2]{0:T(256)(128)(2,1)}, bf16[2]{0:T(256)(128)(2,1)S(1)}, u32[]{:S(2)}, u32[]{:S(2)}) collective-permute-start(bf16[2]{0:T(256)(128)(2,1)} %param.3), channel_id=1, source_target_pairs={{0,2},{2,4},{4,6},{6,8},{8,10},{10,12},{12,14},{14,16},{16,18},{18... | collective-permute-start | bytes 20 | tf_op jit(solution)/shard_map/ppermute | solution.py:36
  9.3 1.9 %convert_multiply_fusion.3 = f32[2,16,4096]{2,1,0:T(8,128)} fusion(bf16[2,16,4096]{2,1,0:T(8,128)(2,1)} %param.2, f32[2]{0:T(128)S(1)} %convert_element_type.76), kind=kLoop, calls=%fused_computation.64 | loop fusion | flops 262144 | bytes 786440 | tf_op jit(solution)/shard_map/mul | solution.py:80
  11.2 1.9 %collective-permute-done.2 = bf16[2]{0:T(256)(128)(2,1)S(1)} collective-permute-done((bf16[2]{0:T(256)(128)(2,1)}, bf16[2]{0:T(256)(128)(2,1)S(1)}, u32[]{:S(2)}, u32[]{:S(2)}) %collective-permute-start.2) | collective-permute-done | bytes 36 | tf_op jit(solution)/shard_map/ppermute | solution.py:36
  13.1 5.7 %collective-permute-done.6 = bf16[2]{0:T(256)(128)(2,1)S(1)} collective-permute-done((bf16[2]{0:T(256)(128)(2,1)S(1)}, bf16[2]{0:T(256)(128)(2,1)S(1)}, u32[]{:S(2)}, u32[]{:S(2)}) %collective-permute-start.6) | collective-permute-done | bytes 36 | tf_op jit(solution)/shard_map/ppermute | solution.py:36
  18.8 5.7 %collective-permute-done.10 = bf16[2]{0:T(256)(128)(2,1)S(1)} collective-permute-done((bf16[2]{0:T(256)(128)(2,1)S(1)}, bf16[2]{0:T(256)(128)(2,1)S(1)}, u32[]{:S(2)}, u32[]{:S(2)}) %collective-permute-start.10) | collective-permute-done | bytes 36 | tf_op jit(solution)/shard_map/ppermute | solution.py:36
  25.7 4.5 %collective-permute-start.4 = (bf16[2,2,4096]{2,1,0:T(2,128)(2,1)S(1)}, bf16[2,2,4096]{2,1,0:T(2,128)(2,1)S(1)}, u32[]{:S(2)}, u32[]{:S(2)}) collective-permute-start(bf16[2,2,4096]{2,1,0:T(2,128)(2,1)S(1)} %get-tuple-element.13), channel_id=1, source_target_pairs={{0,1},{2,3},{4,5},{6,7},{8,9},{10,11},{12,13},{14,15},{16,17},{18,... | collective-permute-start | bytes 98312 | tf_op jit(solution)/shard_map/ppermute | solution.py:28
  32.5 3.5 %collective-permute-done.5 = bf16[2,2,4096]{2,1,0:T(2,128)(2,1)S(1)} collective-permute-done((bf16[2,2,4096]{2,1,0:T(2,128)(2,1)S(1)}, bf16[2,2,4096]{2,1,0:T(2,128)(2,1)S(1)}, u32[]{:S(2)}, u32[]{:S(2)}) %collective-permute-start.5) | collective-permute-done | bytes 32800 | tf_op jit(solution)/shard_map/ppermute | solution.py:29
  36.2 3.9 %collective-permute-done.7 = bf16[2,16,4096]{2,1,0:T(8,128)(2,1)S(1)} collective-permute-done((bf16[2,16,4096]{2,1,0:T(8,128)(2,1)S(1)}, bf16[2,16,4096]{2,1,0:T(8,128)(2,1)S(1)}, u32[]{:S(2)}, u32[]{:S(2)}) %collective-permute-start.7) | collective-permute-done | bytes 262176 | tf_op jit(solution)/shard_map/ppermute | solution.py:36
  40.1 4.5 %collective-permute-start.8 = (bf16[2,2,4096]{2,1,0:T(2,128)(2,1)S(1)}, bf16[2,2,4096]{2,1,0:T(2,128)(2,1)S(1)}, u32[]{:S(2)}, u32[]{:S(2)}) collective-permute-start(bf16[2,2,4096]{2,1,0:T(2,128)(2,1)S(1)} %get-tuple-element.19), channel_id=1, source_target_pairs={{0,1},{2,3},{4,5},{6,7},{8,9},{10,11},{12,13},{14,15},{16,17},{18,... | collective-permute-start | bytes 98312 | tf_op jit(solution)/shard_map/ppermute | solution.py:28
  46.9 3.5 %collective-permute-done.9 = bf16[2,2,4096]{2,1,0:T(2,128)(2,1)S(1)} collective-permute-done((bf16[2,2,4096]{2,1,0:T(2,128)(2,1)S(1)}, bf16[2,2,4096]{2,1,0:T(2,128)(2,1)S(1)}, u32[]{:S(2)}, u32[]{:S(2)}) %collective-permute-start.9) | collective-permute-done | bytes 32800 | tf_op jit(solution)/shard_map/ppermute | solution.py:29
  50.6 3.9 %collective-permute-done.11 = bf16[2,16,4096]{2,1,0:T(8,128)(2,1)S(1)} collective-permute-done((bf16[2,16,4096]{2,1,0:T(8,128)(2,1)S(1)}, bf16[2,16,4096]{2,1,0:T(8,128)(2,1)S(1)}, u32[]{:S(2)}, u32[]{:S(2)}) %collective-permute-start.11) | collective-permute-done | bytes 262176 | tf_op jit(solution)/shard_map/ppermute | solution.py:36
  54.6 4.5 %collective-permute-start.12 = (bf16[2,2,4096]{2,1,0:T(2,128)(2,1)S(1)}, bf16[2,2,4096]{2,1,0:T(2,128)(2,1)S(1)}, u32[]{:S(2)}, u32[]{:S(2)}) collective-permute-start(bf16[2,2,4096]{2,1,0:T(2,128)(2,1)S(1)} %get-tuple-element.15), channel_id=1, source_target_pairs={{0,1},{2,3},{4,5},{6,7},{8,9},{10,11},{12,13},{14,15},{16,17},{18,... | collective-permute-start | bytes 98312 | tf_op jit(solution)/shard_map/ppermute | solution.py:28
  59.1 1.3 %collective-permute-start.13 = (bf16[2,2,4096]{2,1,0:T(2,128)(2,1)S(1)}, bf16[2,2,4096]{2,1,0:T(2,128)(2,1)S(1)}, u32[]{:S(2)}, u32[]{:S(2)}) collective-permute-start(bf16[2,2,4096]{2,1,0:T(2,128)(2,1)S(1)} %get-tuple-element.16), channel_id=1, source_target_pairs={{1,0},{3,2},{5,4},{7,6},{9,8},{11,10},{13,12},{15,14},{17,16},{19,... | collective-permute-start | bytes 98312 | tf_op jit(solution)/shard_map/ppermute | solution.py:29
  61.4 3.6 %collective-permute-done.13 = bf16[2,2,4096]{2,1,0:T(2,128)(2,1)S(1)} collective-permute-done((bf16[2,2,4096]{2,1,0:T(2,128)(2,1)S(1)}, bf16[2,2,4096]{2,1,0:T(2,128)(2,1)S(1)}, u32[]{:S(2)}, u32[]{:S(2)}) %collective-permute-start.13) | collective-permute-done | bytes 32800 | tf_op jit(solution)/shard_map/ppermute | solution.py:29
  65.8 1.3 %slice.279 = f32[2,2,18,4096]{3,2,1,0:T(8,128)} slice(f32[2,2,20,4096]{3,2,1,0:T(8,128)S(1)} %get-tuple-element.12), slice={[0:2], [0:2], [1:19], [0:4096]} | slice | bytes 2359296 | tf_op jit(solution)/shard_map/slice | solution.py:51
  67.1 1.3 %slice.288 = f32[2,2,18,4096]{3,2,1,0:T(8,128)} slice(f32[2,2,20,4096]{3,2,1,0:T(8,128)S(1)} %get-tuple-element.9), slice={[0:2], [0:2], [1:19], [0:4096]} | slice | bytes 2359296 | tf_op jit(solution)/shard_map/slice | solution.py:51
  68.4 1.3 %slice.297 = f32[2,2,18,4096]{3,2,1,0:T(8,128)} slice(f32[2,2,20,4096]{3,2,1,0:T(8,128)S(1)} %get-tuple-element.10), slice={[0:2], [0:2], [1:19], [0:4096]} | slice | bytes 2359296 | tf_op jit(solution)/shard_map/slice | solution.py:51
  69.8 1.4 %slice.306 = f32[2,2,18,4096]{3,2,1,0:T(8,128)} slice(f32[2,2,20,4096]{3,2,1,0:T(8,128)S(1)} %get-tuple-element.11), slice={[0:2], [0:2], [1:19], [0:4096]} | slice | bytes 2359296 | tf_op jit(solution)/shard_map/slice | solution.py:51
  71.1 16.7 %fusion.11 = (f32[2,2,18,4096]{3,2,1,0:T(8,128)S(1)}, f32[2,2,18,4096]{3,2,1,0:T(8,128)S(1)}, f32[2,2,18,4096]{3,2,1,0:T(8,128)S(1)}, f32[2,2,18,4096]{3,2,1,0:T(8,128)}) fusion(f32[2,2,20,4096]{3,2,1,0:T(8,128)S(1)} %get-tuple-element.9, f32[2,2,18,4096]{3,2,1,0:T(8,128)} %slice.288, pred[18]{0:T(512)(128)(4,1)S(1)} %compare_and_fusion, ...), kind=kLoop, calls=%fused_computation.14 | loop fusion | flops 11796480 | bytes 18882578 | tf_op jit(solution)/shard_map/jit(_where)/select_n | solution.py:72
  87.8 1.5 %slice.280 = f32[2,2,16,4096]{3,2,1,0:T(8,128)S(1)} slice(f32[2,2,18,4096]{3,2,1,0:T(8,128)} %get-tuple-element.24), slice={[0:2], [0:2], [1:17], [0:4096]} | slice | bytes 2097152 | tf_op jit(solution)/shard_map/slice | solution.py:74
  91.1 2.4 %fusion.47 = (f32[2,16,4096]{2,1,0:T(8,128)S(1)}, f32[2,16,4096]{2,1,0:T(8,128)S(1)}) fusion(f32[2,2,18,4096]{3,2,1,0:T(8,128)S(1)} %copy-done, f32[2,2,16,4096]{3,2,1,0:T(8,128)S(1)} %slice.280, f32[2,2,20,4096]{3,2,1,0:T(8,128)S(1)} %get-tuple-element.12, f32[2,16,4096]{2,1,0:T(8,128)S(1)} %copy-done.1, pred[4096]{0:T(1024)(128)(4,1)S(1)} %get-tuple-element.25, ...), kind=kLoop, calls=%fused_computation.55 | loop fusion | flops 8650752 | bytes 10493952 | tf_op jit(solution)/shard_map/reduce_sum | solution.py:79
  93.6 2.4 %fusion.31 = (f32[2,16,4096]{2,1,0:T(8,128)S(1)}, f32[2,16,4096]{2,1,0:T(8,128)S(1)}) fusion(f32[2,2,18,4096]{3,2,1,0:T(8,128)S(1)} %get-tuple-element.22, f32[2,2,16,4096]{3,2,1,0:T(8,128)S(1)} %slice.298, f32[2,2,20,4096]{3,2,1,0:T(8,128)S(1)} %get-tuple-element.10, f32[2,16,4096]{2,1,0:T(8,128)S(1)} %copy-done.3, ...), kind=kLoop, calls=%fused_computation.37 | loop fusion | flops 8650752 | bytes 10493952 | tf_op jit(solution)/shard_map/reduce_sum | solution.py:79
  (45 shorter events, 12.8 us)
Async XLA Ops:
  0.0 25.6 %collective-permute-start.3 = (bf16[2,16,4096]{2,1,0:T(8,128)(2,1)}, bf16[2,16,4096]{2,1,0:T(8,128)(2,1)S(1)}, u32[]{:S(2)}, u32[]{:S(2)}) collective-permute-start(bf16[2,16,4096]{2,1,0:T(8,128)(2,1)} %param.2), channel_id=1, source_target_pairs={{0,2},{2,4},{4,6},{6,8},{8,10},{10,12},{12,14},{14,16},{16,18},{18... | collective-permute-start | bytes 786440 | tf_op jit(solution)/shard_map/ppermute | solution.py:36
  1.5 23.0 %collective-permute-start = (bf16[2,2,4096]{2,1,0:T(2,128)(2,1)S(1)}, bf16[2,2,4096]{2,1,0:T(2,128)(2,1)S(1)}, u32[]{:S(2)}, u32[]{:S(2)}) collective-permute-start(bf16[2,2,4096]{2,1,0:T(2,128)(2,1)S(1)} %get-tuple-element.17), channel_id=1, source_target_pairs={{0,1},{2,3},{4,5},{6,7},{8,9},{10,11},{12,13},{14,15},{16,17},{18,... | collective-permute-start | bytes 98312 | tf_op jit(solution)/shard_map/ppermute | solution.py:28
  5.9 18.6 %collective-permute-start.1 = (bf16[2,2,4096]{2,1,0:T(2,128)(2,1)S(1)}, bf16[2,2,4096]{2,1,0:T(2,128)(2,1)S(1)}, u32[]{:S(2)}, u32[]{:S(2)}) collective-permute-start(bf16[2,2,4096]{2,1,0:T(2,128)(2,1)S(1)} %get-tuple-element.18), channel_id=1, source_target_pairs={{1,0},{3,2},{5,4},{7,6},{9,8},{11,10},{13,12},{15,14},{17,16},{19,... | collective-permute-start | bytes 98312 | tf_op jit(solution)/shard_map/ppermute | solution.py:29
  7.2 5.9 %collective-permute-start.2 = (bf16[2]{0:T(256)(128)(2,1)}, bf16[2]{0:T(256)(128)(2,1)S(1)}, u32[]{:S(2)}, u32[]{:S(2)}) collective-permute-start(bf16[2]{0:T(256)(128)(2,1)} %param.3), channel_id=1, source_target_pairs={{0,2},{2,4},{4,6},{6,8},{8,10},{10,12},{12,14},{14,16},{16,18},{18... | collective-permute-start | bytes 20 | tf_op jit(solution)/shard_map/ppermute | solution.py:36
  13.1 5.7 %collective-permute-start.6 = (bf16[2]{0:T(256)(128)(2,1)S(1)}, bf16[2]{0:T(256)(128)(2,1)S(1)}, u32[]{:S(2)}, u32[]{:S(2)}) collective-permute-start(bf16[2]{0:T(256)(128)(2,1)S(1)} %collective-permute-done.2), channel_id=1, source_target_pairs={{0,2},{2,4},{4,6},{6,8},{8,10},{10,12},{12,14},{14,16},{16,18},{18... | collective-permute-start | bytes 20 | tf_op jit(solution)/shard_map/ppermute | solution.py:36
  18.8 5.7 %collective-permute-start.10 = (bf16[2]{0:T(256)(128)(2,1)S(1)}, bf16[2]{0:T(256)(128)(2,1)S(1)}, u32[]{:S(2)}, u32[]{:S(2)}) collective-permute-start(bf16[2]{0:T(256)(128)(2,1)S(1)} %collective-permute-done.6), channel_id=1, source_target_pairs={{0,2},{2,4},{4,6},{6,8},{8,10},{10,12},{12,14},{14,16},{16,18},{18... | collective-permute-start | bytes 20 | tf_op jit(solution)/shard_map/ppermute | solution.py:36
  25.7 6.8 %collective-permute-start.4 = (bf16[2,2,4096]{2,1,0:T(2,128)(2,1)S(1)}, bf16[2,2,4096]{2,1,0:T(2,128)(2,1)S(1)}, u32[]{:S(2)}, u32[]{:S(2)}) collective-permute-start(bf16[2,2,4096]{2,1,0:T(2,128)(2,1)S(1)} %get-tuple-element.13), channel_id=1, source_target_pairs={{0,1},{2,3},{4,5},{6,7},{8,9},{10,11},{12,13},{14,15},{16,17},{18,... | collective-permute-start | bytes 98312 | tf_op jit(solution)/shard_map/ppermute | solution.py:28
  30.2 5.8 %collective-permute-start.5 = (bf16[2,2,4096]{2,1,0:T(2,128)(2,1)S(1)}, bf16[2,2,4096]{2,1,0:T(2,128)(2,1)S(1)}, u32[]{:S(2)}, u32[]{:S(2)}) collective-permute-start(bf16[2,2,4096]{2,1,0:T(2,128)(2,1)S(1)} %get-tuple-element.14), channel_id=1, source_target_pairs={{1,0},{3,2},{5,4},{7,6},{9,8},{11,10},{13,12},{15,14},{17,16},{19,... | collective-permute-start | bytes 98312 | tf_op jit(solution)/shard_map/ppermute | solution.py:29
  31.5 8.5 %collective-permute-start.7 = (bf16[2,16,4096]{2,1,0:T(8,128)(2,1)S(1)}, bf16[2,16,4096]{2,1,0:T(8,128)(2,1)S(1)}, u32[]{:S(2)}, u32[]{:S(2)}) collective-permute-start(bf16[2,16,4096]{2,1,0:T(8,128)(2,1)S(1)} %collective-permute-done.3), channel_id=1, source_target_pairs={{0,2},{2,4},{4,6},{6,8},{8,10},{10,12},{12,14},{14,16},{16,18},{18... | collective-permute-start | bytes 786440 | tf_op jit(solution)/shard_map/ppermute | solution.py:36
  40.1 6.8 %collective-permute-start.8 = (bf16[2,2,4096]{2,1,0:T(2,128)(2,1)S(1)}, bf16[2,2,4096]{2,1,0:T(2,128)(2,1)S(1)}, u32[]{:S(2)}, u32[]{:S(2)}) collective-permute-start(bf16[2,2,4096]{2,1,0:T(2,128)(2,1)S(1)} %get-tuple-element.19), channel_id=1, source_target_pairs={{0,1},{2,3},{4,5},{6,7},{8,9},{10,11},{12,13},{14,15},{16,17},{18,... | collective-permute-start | bytes 98312 | tf_op jit(solution)/shard_map/ppermute | solution.py:28
  44.7 5.8 %collective-permute-start.9 = (bf16[2,2,4096]{2,1,0:T(2,128)(2,1)S(1)}, bf16[2,2,4096]{2,1,0:T(2,128)(2,1)S(1)}, u32[]{:S(2)}, u32[]{:S(2)}) collective-permute-start(bf16[2,2,4096]{2,1,0:T(2,128)(2,1)S(1)} %get-tuple-element.20), channel_id=1, source_target_pairs={{1,0},{3,2},{5,4},{7,6},{9,8},{11,10},{13,12},{15,14},{17,16},{19,... | collective-permute-start | bytes 98312 | tf_op jit(solution)/shard_map/ppermute | solution.py:29
  46.0 8.5 %collective-permute-start.11 = (bf16[2,16,4096]{2,1,0:T(8,128)(2,1)S(1)}, bf16[2,16,4096]{2,1,0:T(8,128)(2,1)S(1)}, u32[]{:S(2)}, u32[]{:S(2)}) collective-permute-start(bf16[2,16,4096]{2,1,0:T(8,128)(2,1)S(1)} %collective-permute-done.7), channel_id=1, source_target_pairs={{0,2},{2,4},{4,6},{6,8},{8,10},{10,12},{12,14},{14,16},{16,18},{18... | collective-permute-start | bytes 786440 | tf_op jit(solution)/shard_map/ppermute | solution.py:36
  54.6 6.8 %collective-permute-start.12 = (bf16[2,2,4096]{2,1,0:T(2,128)(2,1)S(1)}, bf16[2,2,4096]{2,1,0:T(2,128)(2,1)S(1)}, u32[]{:S(2)}, u32[]{:S(2)}) collective-permute-start(bf16[2,2,4096]{2,1,0:T(2,128)(2,1)S(1)} %get-tuple-element.15), channel_id=1, source_target_pairs={{0,1},{2,3},{4,5},{6,7},{8,9},{10,11},{12,13},{14,15},{16,17},{18,... | collective-permute-start | bytes 98312 | tf_op jit(solution)/shard_map/ppermute | solution.py:28
  59.1 5.8 %collective-permute-start.13 = (bf16[2,2,4096]{2,1,0:T(2,128)(2,1)S(1)}, bf16[2,2,4096]{2,1,0:T(2,128)(2,1)S(1)}, u32[]{:S(2)}, u32[]{:S(2)}) collective-permute-start(bf16[2,2,4096]{2,1,0:T(2,128)(2,1)S(1)} %get-tuple-element.16), channel_id=1, source_target_pairs={{1,0},{3,2},{5,4},{7,6},{9,8},{11,10},{13,12},{15,14},{17,16},{19,... | collective-permute-start | bytes 98312 | tf_op jit(solution)/shard_map/ppermute | solution.py:29
  89.4 1.0 %copy-start.2 = (f32[2,16,4096]{2,1,0:T(8,128)S(1)}, f32[2,16,4096]{2,1,0:T(8,128)}, u32[]{:S(2)}) copy-start(f32[2,16,4096]{2,1,0:T(8,128)} %convert_multiply_fusion.2) | copy-start | bytes 1572868
  89.5 1.5 %copy-start = (f32[2,2,18,4096]{3,2,1,0:T(8,128)S(1)}, f32[2,2,18,4096]{3,2,1,0:T(8,128)}, u32[]{:S(2)}) copy-start(f32[2,2,18,4096]{3,2,1,0:T(8,128)} %get-tuple-element.24) | copy-start | bytes 3538948
  89.6 1.6 %copy-start.1 = (f32[2,16,4096]{2,1,0:T(8,128)S(1)}, f32[2,16,4096]{2,1,0:T(8,128)}, u32[]{:S(2)}) copy-start(f32[2,16,4096]{2,1,0:T(8,128)} %convert_multiply_fusion.3) | copy-start | bytes 1572868
  91.1 2.4 %copy-start.3 = (f32[2,16,4096]{2,1,0:T(8,128)S(1)}, f32[2,16,4096]{2,1,0:T(8,128)}, u32[]{:S(2)}) copy-start(f32[2,16,4096]{2,1,0:T(8,128)} %convert_multiply_fusion.1) | copy-start | bytes 1572868
  91.1 2.4 %copy-start.4 = (f32[2,16,4096]{2,1,0:T(8,128)S(1)}, f32[2,16,4096]{2,1,0:T(8,128)}, u32[]{:S(2)}) copy-start(f32[2,16,4096]{2,1,0:T(8,128)} %convert_multiply_fusion) | copy-start | bytes 1572868
where the time goes:
time: 97.3 us; the launch traced here: 96.9 us
  waiting for transfers between devices  31.7 us (33%)
  other arithmetic  30 us (31%)
  starting transfers between devices  25.2 us (26%)
  local copies, waits for them, and re-layouts  9.71 us (10%)
    ppermute x6, waiting for transfers between devices, passed_along(): lax.ppermute(array, axis, [(i, (i + by) % size) for i in range(size)])  21 us
    ppermute x4, starting transfers between devices, with_halo(): before = lax.ppermute(last, axis, up)  18 us
    select_n x1, other arithmetic, per_device(): first_wide = jnp.where(inside[:, None], first_wide, 0.0)  16.7 us
    ppermute x4, waiting for transfers between devices, with_halo(): after = lax.ppermute(leading, axis, down)  10.6 us
    slice x4, local copies, waits for them, and re-layouts, neighbour_planes(): extended[:, :, 1:-1]  5.27 us
    ppermute x4, starting transfers between devices, with_halo(): after = lax.ppermute(leading, axis, down)  5.17 us
    reduce_sum x2, other arithmetic, per_device(): jnp.sum(weights[None, :, None, None] * visitor[None] * potential, axis=1)  4.81 us
    mul x4, other arithmetic, per_device(): weights[None, :, None, None] * visitor[None] * potential  4.66 us
  transfers between devices with their start and end apart: 14, of which 8 were waited for; matrix products, arithmetic and copies ran while one was open for 8% of the time, Pallas kernels for 0%

commit v1 on v0

v1 whole, which is shorter than its diff:
```python
import functools
import math

import jax
import jax.numpy as jnp
from jax import lax
from jax.experimental import pallas as pl
from jax.experimental.pallas import tpu as pltpu
from jax.sharding import PartitionSpec as P

NZ = 64
STEPS = 3
LANES = 128
WIDTH = 2
UNROLL = 4
MESH = pl.DeviceIdType.MESH


screening = 0.5
ratio_mid = (12.0 + 2.0 * screening) / 12.0
root_term = math.sqrt(ratio_mid * ratio_mid - 1.0)
decay_ratio = ratio_mid - root_term
coeff_zero = 1.0 / (6.0 * root_term)
coeff_one = -2.0 * decay_ratio * coeff_zero
coeff_two = 2.0 * decay_ratio * decay_ratio * coeff_zero

scale = coeff_two / 18.0
inner = -coeff_one / 6.0 / scale
outer = (coeff_zero - coeff_two) / scale


def loop(count, body, unroll=1):
    lax.fori_loop(0, count, lambda i, c: (body(i), c)[1], 0, unroll=unroll)


def lane_tile(t):
    return pl.ds(pl.multiple_of(t * LANES, LANES), LANES)


def kernel(n_band, n_slab, orb_ref, occ_ref, out_ref, block, slots, edges, halos, own, vis,
           weighted, dens, inner_field, load_sem, send_sem, recv_sem, edge_send, edge_recv):
    orbs, planes, cells = orb_ref.shape
    tiles = cells // LANES
    ext = vis.shape[2]
    band, slab = lax.axis_index("band"), lax.axis_index("slab")
    odd = lax.rem(band, 2)

    def at(by, side=0):
        return {"band": lax.rem(band + by + n_band, n_band), "slab": slab + side}

    sibling = at(1 - 2 * odd)
    has = (slab > 0, slab < n_slab - 1)
    step_of = (-1, 1)

    load = pltpu.make_async_copy(orb_ref, block.at[:, :, :cells], load_sem.at[0])
    load_occ = pltpu.make_async_copy(occ_ref, block.at[:, :, cells:], load_sem.at[1])
    load.start()
    load_occ.start()

    barrier = pltpu.get_barrier_semaphore()
    pl.semaphore_signal(barrier, inc=1, device_id=at(-2), device_id_type=MESH)
    pl.semaphore_signal(barrier, inc=1, device_id=at(2 * odd - 3), device_id_type=MESH)
    pl.semaphore_signal(barrier, inc=1, device_id=sibling, device_id_type=MESH)
    for side in range(2):
        @pl.when(has[side])
        def _(side=side):
            for s in range(STEPS + 1):
                pl.semaphore_signal(barrier, inc=1, device_id=at(-s, step_of[side]), device_id_type=MESH)

    load.wait()
    load_occ.wait()

    def cut(k):
        parts = ([], [])
        for h in range(2):
            for o in range(orbs):
                tile = block[o, :, lane_tile(2 * k + h)].astype(jnp.float32)
                parts[0].append(tile[:WIDTH])
                parts[1].append(tile[planes - WIDTH:])
        for side in range(2):
            edges[side, k] = jnp.concatenate(parts[side], axis=0).astype(jnp.bfloat16)

    loop(tiles // 2, cut, 2)

    for side in range(2):
        @pl.when(jnp.logical_not(has[side]))
        def _(side=side):
            halos[:, side] = jnp.zeros(halos.shape[:1] + halos.shape[2:], jnp.bfloat16)

    sides = has[0].astype(jnp.int32) + has[1].astype(jnp.int32)
    pl.semaphore_wait(barrier, 3 + (STEPS + 1) * sides)

    def edge_copy(side, s):
        return pltpu.make_async_remote_copy(
            src_ref=edges.at[side], dst_ref=halos.at[s, 1 - side],
            send_sem=edge_send.at[s, side], recv_sem=edge_recv.at[s, 1 - side],
            device_id=at(s, step_of[side]), device_id_type=MESH)

    def edge_wait(side, s):
        return pltpu.make_async_remote_copy(
            src_ref=edges.at[1 - side], dst_ref=halos.at[s, side],
            send_sem=edge_send.at[s, 1 - side], recv_sem=edge_recv.at[s, side],
            device_id=at(s, step_of[side]), device_id_type=MESH)

    def block_copy(src, slot, to):
        return pltpu.make_async_remote_copy(
            src_ref=src, dst_ref=slots.at[slot], send_sem=send_sem.at[slot],
            recv_sem=recv_sem.at[slot], device_id=to, device_id_type=MESH)

    def send_edges(steps):
        for side in range(2):
            @pl.when(has[side])
            def _(side=side):
                for s in steps:
                    edge_copy(side, s).start()

    direct = block_copy(block, 0, at(1 + 2 * odd))
    second = block_copy(block, 1, at(2))
    passed = block_copy(slots.at[1], 2, sibling)
    send_edges((0,))
    second.start()
    direct.start()
    send_edges(range(1, STEPS + 1))

    for p in range(orbs * orbs):
        for t in (0, tiles + 1):
            dens[p, t] = jnp.zeros(dens.shape[2:], jnp.float32)
            inner_field[p, t] = jnp.zeros(inner_field.shape[2:], jnp.float32)

    lane = lax.broadcasted_iota(jnp.int32, (1, LANES), 1)
    high = lane >= NZ
    column = lane % NZ
    first_col, last_col = column == 0, column == NZ - 1
    row = lax.broadcasted_iota(jnp.int32, (ext, LANES), 0)
    below = jnp.where(has[0], 1.0, 0.0)
    above = jnp.where(has[1], 1.0, 0.0)
    row_mask = jnp.where(row == 0, below, jnp.where(row == planes + 1, above, 1.0))

    def across(mid, before, after):
        pairs = pltpu.roll(mid + jnp.where(high, before, after), NZ, 1)
        left = pltpu.roll(jnp.where(last_col, 0.0, mid), 1, 1)
        right = pltpu.roll(jnp.where(first_col, 0.0, mid), LANES - 1, 1)
        return pairs + (left + right)

    def widen(src, low, up, dst):
        def body(k):
            lo = low[k].astype(jnp.float32)
            hi = up[k].astype(jnp.float32)
            for h in range(2):
                for o in range(orbs):
                    t = 2 * k + h
                    r = (h * orbs + o) * WIDTH
                    dst[o, t, :WIDTH] = lo[r:r + WIDTH]
                    dst[o, t, planes + WIDTH:planes + 2 * WIDTH] = hi[r:r + WIDTH]
                    dst[o, t, WIDTH:planes + WIDTH] = src[o, :, lane_tile(t)].astype(jnp.float32)
        loop(tiles // 2, body, 2)

    def visit(src, other, first):
        weights = [-scale * src[o, :, cells:].astype(jnp.float32) for o in range(orbs)]

        def density(t):
            for o in range(orbs):
                weighted[o, t] = weights[o] * other[o, t, WIDTH:planes + WIDTH]
            for i in range(orbs):
                for j in range(orbs):
                    dens[i * orbs + j, t + 1, :ext] = own[i, t] * other[j, t]

        def once(t):
            for p in range(orbs * orbs):
                mid = dens[p, t + 1, 1:ext + 1]
                along = dens[p, t + 1, :ext] + dens[p, t + 1, 2:ext + 2]
                u = inner * mid + along + across(mid, dens[p, t, 1:ext + 1], dens[p, t + 2, 1:ext + 1])
                inner_field[p, t + 1] = u * row_mask

        def twice(t):
            for i in range(orbs):
                total = None
                for j in range(orbs):
                    p = i * orbs + j
                    mid = inner_field[p, t + 1, 1:planes + 1]
                    along = inner_field[p, t + 1, :planes] + inner_field[p, t + 1, 2:planes + 2]
                    v = along + across(mid, inner_field[p, t, 1:planes + 1], inner_field[p, t + 2, 1:planes + 1])
                    v = v + outer * dens[p, t + 1, WIDTH:planes + WIDTH]
                    term = weighted[j, t] * v
                    total = term if total is None else total + term
                if not first:
                    total = total + out_ref[i, :, lane_tile(t)]
                out_ref[i, :, lane_tile(t)] = total

        loop(tiles, density, UNROLL)
        loop(tiles, once, UNROLL)
        loop(tiles, twice, UNROLL)

    def wait_halos(s):
        for side in range(2):
            @pl.when(has[side])
            def _(side=side):
                edge_wait(side, s).wait_recv()

    wait_halos(0)
    widen(block, halos.at[0, 0], halos.at[0, 1], own)
    visit(block, own, True)

    second.wait_recv()
    passed.start()
    wait_halos(2)
    widen(slots.at[1], halos.at[2, 0], halos.at[2, 1], vis)
    visit(slots.at[1], vis, False)

    wait_halos(1)
    wait_halos(3)
    for slot, wait, step in ((0, direct, 3 - 2 * odd), (2, passed, 1 + 2 * odd)):
        wait.wait_recv()
        widen(slots.at[slot], halos.at[step, 0], halos.at[step, 1], vis)
        visit(slots.at[slot], vis, False)

    direct.wait_send()
    second.wait_send()
    passed.wait_send()
    for side in range(2):
        @pl.when(has[side])
        def _(side=side):
            for s in range(STEPS + 1):
                edge_copy(side, s).wait_send()


def per_device(n_band, n_slab, orbitals, occupation):
    orbs, planes, cells = orbitals.shape
    tiles = cells // LANES
    ext = -(-(planes + 2 * WIDTH) // 8) * 8
    occ = jnp.broadcast_to(occupation[:, None, None], (orbs, planes, LANES))
    f32, bf16 = jnp.float32, jnp.bfloat16
    rows = 2 * orbs * WIDTH
    return pl.pallas_call(
        functools.partial(kernel, n_band, n_slab),
        out_shape=jax.ShapeDtypeStruct(orbitals.shape, f32),
        in_specs=[pl.BlockSpec(memory_space=pl.ANY)] * 2,
        out_specs=pl.BlockSpec(memory_space=pltpu.VMEM),
        scratch_shapes=[
            pltpu.VMEM((orbs, planes, cells + LANES), bf16),
            pltpu.VMEM((STEPS, orbs, planes, cells + LANES), bf16),
            pltpu.VMEM((2, tiles // 2, rows, LANES), bf16),
            pltpu.VMEM((STEPS + 1, 2, tiles // 2, rows, LANES), bf16),
            pltpu.VMEM((orbs, tiles, ext, LANES), f32),
            pltpu.VMEM((orbs, tiles, ext, LANES), f32),
            pltpu.VMEM((orbs, tiles, planes, LANES), f32),
            pltpu.VMEM((orbs * orbs, tiles + 2, ext + 8, LANES), f32),
            pltpu.VMEM((orbs * orbs, tiles + 2, ext, LANES), f32),
            pltpu.SemaphoreType.DMA((2,)),
            pltpu.SemaphoreType.DMA((STEPS,)),
            pltpu.SemaphoreType.DMA((STEPS,)),
            pltpu.SemaphoreType.DMA((STEPS + 1, 2)),
            pltpu.SemaphoreType.DMA((STEPS + 1, 2)),
        ],
        compiler_params=pltpu.CompilerParams(collective_id=0, has_side_effects=True),
        name="exchange",
    )(orbitals, occ)


def solution(mesh):
    in_specs = (P("band", "slab", None), P("band"))
    out_specs = P("band", "slab", None)
    return jax.shard_map(
        functools.partial(per_device, mesh.shape["band"], mesh.shape["slab"]),
        mesh=mesh, in_specs=in_specs, out_specs=out_specs, check_vma=False,
    )
```

time: 97.3 us -> 32.8 us (0.34)
  the two profiles are of different devices: /device:TPU:0 before, /device:TPU:1 now
where the time goes in v1:
time: 32.8 us; the launch traced here: 32.7 us
  Pallas kernels  29.5 us (90%)
  local copies, waits for them, and re-layouts  3.19 us (10%)
    pallas_call x1, Pallas kernels, per_device(): pl.pallas_call(functools.partial(kernel, n_band, n_slab), out_shape=jax.S...  29.5 us
    unnamed x1, local copies, waits for them, and re-layouts  1.87 us
    broadcast_in_dim x1, local copies, waits for them, and re-layouts, per_device(): occ = jnp.broadcast_to(occupation[:, None, None], (orbs, planes, LANES))  1.32 us

profile of v1, /device:TPU:1, one launch (start us, length us, event | category | flops | bytes accessed | tf_op | source)
XLA Modules:
  0.0 32.7 jit_solution(9634574643098082404)
XLA Ops:
  0.0 1.3 %broadcast_in_dim.2.occ_ref = bf16[2,16,128]{2,1,0:T(8,128)(2,1)} broadcast(bf16[2]{0:T(256)(128)(2,1)} %param.3), dimensions={0} | broadcast | bytes 8196 | tf_op jit(solution)/shard_map/broadcast_in_dim | solution.py:231
  1.3 29.5 %exchange.1 = f32[2,16,4096]{2,1,0:T(8,128)} custom-call(bf16[2,16,4096]{2,1,0:T(8,128)(2,1)} %orb_ref.1, bf16[2,16,128]{2,1,0:T(8,128)(2,1)} %broadcast_in_dim.2.occ_ref), custom_call_target="tpu_custom_call" | custom-call | tf_op jit(solution)/shard_map/exchange/pallas_call | solution.py:234
  30.8 1.9 %copy.4 = f32[2,16,4096]{2,1,0:T(8,128)} copy(f32[2,16,4096]{2,1,0:T(8,128)} %exchange.1) | data formatting | bytes 1048576

commit v2 on v1

v2 whole, which is shorter than its diff:
```python
import functools
import math

import jax
import jax.numpy as jnp
from jax import lax
from jax.experimental import pallas as pl
from jax.experimental.pallas import tpu as pltpu
from jax.sharding import PartitionSpec as P

NZ = 64
STEPS = 3
LANES = 128
WIDTH = 2
UNROLL = 4
MESH = pl.DeviceIdType.MESH


screening = 0.5
ratio_mid = (12.0 + 2.0 * screening) / 12.0
root_term = math.sqrt(ratio_mid * ratio_mid - 1.0)
decay_ratio = ratio_mid - root_term
coeff_zero = 1.0 / (6.0 * root_term)
coeff_one = -2.0 * decay_ratio * coeff_zero
coeff_two = 2.0 * decay_ratio * decay_ratio * coeff_zero

scale = coeff_two / 18.0
inner = -coeff_one / 6.0 / scale
outer = (coeff_zero - coeff_two) / scale


def loop(count, body, unroll=1):
    lax.fori_loop(0, count, lambda i, c: (body(i), c)[1], 0, unroll=unroll)


def lane_tile(t):
    return pl.ds(pl.multiple_of(t * LANES, LANES), LANES)


def kernel(n_band, n_slab, orb_ref, occ_ref, out_ref, slots, edges, halos, own, own_moved, vis,
           weighted, dens, turned, part, inner_field, load_sem, send_sem, recv_sem, edge_send, edge_recv):
    orbs, planes, cells = orb_ref.shape
    tiles = cells // LANES
    ext = vis.shape[1]
    mine = STEPS
    band, slab = lax.axis_index("band"), lax.axis_index("slab")
    odd = lax.rem(band, 2)

    def at(by, side=0):
        return {"band": lax.rem(band + by + n_band, n_band), "slab": slab + side}

    sibling = at(1 - 2 * odd)
    has = (slab > 0, slab < n_slab - 1)
    step_of = (-1, 1)
    reach = {mine: 0, 1: 2, 0: 1 + 2 * odd}
    source = {mine: 0, 1: -2, 0: 2 * odd - 3}

    load = pltpu.make_async_copy(orb_ref, slots.at[mine, :, :, :cells], load_sem.at[0])
    load_occ = pltpu.make_async_copy(occ_ref, slots.at[mine, :, :, cells:], load_sem.at[1])
    load.start()
    load_occ.start()

    barrier = pltpu.get_barrier_semaphore()
    for by in (source[1], source[0]):
        pl.semaphore_signal(barrier, inc=1, device_id=at(by), device_id_type=MESH)
    pl.semaphore_signal(barrier, inc=1, device_id=sibling, device_id_type=MESH)
    for side in range(2):
        @pl.when(has[side])
        def _(side=side):
            for slot in (mine, 1, 0):
                pl.semaphore_signal(barrier, inc=1, device_id=at(source[slot], step_of[side]), device_id_type=MESH)

    load.wait()
    load_occ.wait()

    def cut(k):
        parts = ([], [])
        for h in range(2):
            for o in range(orbs):
                tile = slots[mine, o, :, lane_tile(2 * k + h)].astype(jnp.float32)
                parts[0].append(tile[:WIDTH])
                parts[1].append(tile[planes - WIDTH:])
        for side in range(2):
            edges[side, k] = jnp.concatenate(parts[side], axis=0).astype(jnp.bfloat16)

    loop(tiles // 2, cut, 2)

    for side in range(2):
        @pl.when(jnp.logical_not(has[side]))
        def _(side=side):
            halos[:, side] = jnp.zeros(halos.shape[:1] + halos.shape[2:], jnp.bfloat16)

    sides = has[0].astype(jnp.int32) + has[1].astype(jnp.int32)
    pl.semaphore_wait(barrier, 3 + 3 * sides)

    def edge_copy(side, slot):
        return pltpu.make_async_remote_copy(
            src_ref=edges.at[side], dst_ref=halos.at[slot, 1 - side],
            send_sem=edge_send.at[slot, side], recv_sem=edge_recv.at[slot, 1 - side],
            device_id=at(reach[slot], step_of[side]), device_id_type=MESH)

    def edge_pass(side):
        return pltpu.make_async_remote_copy(
            src_ref=halos.at[1, side], dst_ref=halos.at[2, side],
            send_sem=edge_send.at[2, side], recv_sem=edge_recv.at[2, side],
            device_id=sibling, device_id_type=MESH)

    def edge_wait(side, slot):
        pltpu.make_async_remote_copy(
            src_ref=edges.at[1 - side], dst_ref=halos.at[slot, side],
            send_sem=edge_send.at[slot, 1 - side], recv_sem=edge_recv.at[slot, side],
            device_id=sibling, device_id_type=MESH).wait_recv()

    def block_copy(slot, o):
        return pltpu.make_async_remote_copy(
            src_ref=slots.at[mine, o], dst_ref=slots.at[slot, o], send_sem=send_sem.at[slot, o],
            recv_sem=recv_sem.at[slot, o], device_id=at(reach[slot]), device_id_type=MESH)

    def block_pass(o):
        return pltpu.make_async_remote_copy(
            src_ref=slots.at[1, o], dst_ref=slots.at[2, o], send_sem=send_sem.at[2, o],
            recv_sem=recv_sem.at[2, o], device_id=sibling, device_id_type=MESH)

    def each_side(action):
        for side in range(2):
            pl.when(has[side])(functools.partial(action, side))

    each_side(lambda side: edge_copy(side, mine).start())
    each_side(lambda side: edge_copy(side, 1).start())
    each_side(lambda side: edge_copy(side, 0).start())
    for o in range(orbs):
        block_copy(1, o).start()
        block_copy(0, o).start()

    for i in range(orbs):
        for t in (0, tiles + 1):
            turned[i, t] = jnp.zeros(turned.shape[2:], jnp.float32)
            inner_field[i, t] = jnp.zeros(inner_field.shape[2:], jnp.float32)

    lane = lax.broadcasted_iota(jnp.int32, (1, LANES), 1)
    high = lane >= NZ
    column = lane % NZ
    first_col, last_col = column == 0, column == NZ - 1
    row = lax.broadcasted_iota(jnp.int32, (ext, LANES), 0)
    below = jnp.where(has[0], 1.0, 0.0)
    above = jnp.where(has[1], 1.0, 0.0)
    row_mask = jnp.where(row == WIDTH - 1, below, jnp.where(row == planes + WIDTH, above, 1.0))

    def from_left(mid):
        return pltpu.roll(jnp.where(last_col, 0.0, mid), 1, 1)

    def from_right(mid):
        return pltpu.roll(jnp.where(first_col, 0.0, mid), LANES - 1, 1)

    def widen(slot, o, dst):
        def body(k):
            low = halos[slot, 0, k].astype(jnp.float32)
            up = halos[slot, 1, k].astype(jnp.float32)
            for h in range(2):
                t = 2 * k + h
                for q in range(orbs):
                    @pl.when(o == q)
                    def _(q=q, h=h, t=t):
                        r = (h * orbs + q) * WIDTH
                        dst[t, :WIDTH] = low[r:r + WIDTH]
                        dst[t, planes + WIDTH:planes + 2 * WIDTH] = up[r:r + WIDTH]
                dst[t, WIDTH:planes + WIDTH] = slots[slot, o, :, lane_tile(t)].astype(jnp.float32)
        loop(tiles // 2, body, 2)

    def visit(slot, o):
        weight = -scale * slots[slot, o, :, cells:].astype(jnp.float32)
        widen(slot, o, vis)

        def density(t):
            mid = vis[t]
            moved = (pltpu.roll(mid, NZ, 1), from_left(mid), from_right(mid))
            weighted[t] = weight * vis[t, WIDTH:planes + WIDTH]
            for i in range(orbs):
                d = own[i, t] * mid
                dens[i, t, 8:ext + 8] = d
                turn = own_moved[i, 0, t] * moved[0]
                turned[i, t + 1] = turn
                part[i, t] = inner * d + turn + (own_moved[i, 1, t] * moved[1] + own_moved[i, 2, t] * moved[2])

        def once(t):
            for i in range(orbs):
                along = dens[i, t, 7:ext + 7] + dens[i, t, 9:ext + 9]
                u = part[i, t] + along + jnp.where(high, turned[i, t + 2], turned[i, t])
                inner_field[i, t + 1] = u * row_mask

        def twice(t):
            for i in range(orbs):
                mid = inner_field[i, t + 1, WIDTH:planes + WIDTH]
                before = inner_field[i, t, WIDTH:planes + WIDTH]
                after = inner_field[i, t + 2, WIDTH:planes + WIDTH]
                v = inner_field[i, t + 1, WIDTH - 1:planes + WIDTH - 1] + inner_field[i, t + 1, WIDTH + 1:planes + WIDTH + 1]
                v = v + pltpu.roll(mid + jnp.where(high, before, after), NZ, 1)
                v = v + (from_left(mid) + from_right(mid))
                v = v + outer * dens[i, t, 8 + WIDTH:8 + planes + WIDTH]
                out_ref[i, :, lane_tile(t)] += weighted[t] * v

        loop(tiles, density, UNROLL)
        loop(tiles, once, UNROLL)
        loop(tiles, twice, UNROLL)

    each_side(lambda side: edge_wait(side, mine))
    for i in range(orbs):
        widen(mine, i, own.at[i])

    def prepare(t):
        for i in range(orbs):
            mid = own[i, t]
            own_moved[i, 0, t] = pltpu.roll(mid, NZ, 1)
            own_moved[i, 1, t] = from_left(mid)
            own_moved[i, 2, t] = from_right(mid)
            out_ref[i, :, lane_tile(t)] = jnp.zeros((planes, LANES), jnp.float32)

    loop(tiles, prepare, UNROLL)

    if_odd, if_even = [(mine, o) for o in range(orbs)], [(mine, o) for o in range(orbs)]
    if_odd += [(0, o) for o in range(orbs)]
    for o in range(orbs):
        if_odd += [(1, o), (2, o)]
        if_even += [(1, o), (0, o), (2, o)]

    def entry(k, column):
        value = jnp.int32(0)
        for n, (a, b) in enumerate(zip(if_odd, if_even)):
            value = jnp.where(k == n, jnp.where(odd == 1, a[column], b[column]), value)
        return value

    def step(k):
        slot, o = entry(k, 0), entry(k, 1)
        for q in range(STEPS):
            for p in range(orbs):
                @pl.when(jnp.logical_and(slot == q, o == p))
                def _(q=q, p=p):
                    if p == 0:
                        each_side(lambda side: edge_wait(side, q))
                        if q == 1:
                            each_side(lambda side: edge_pass(side).start())
                    (block_pass(p) if q == 2 else block_copy(q, p)).wait_recv()
                    if q == 1:
                        block_pass(p).start()
        visit(slot, o)

    loop(len(if_odd), step)

    for o in range(orbs):
        block_copy(0, o).wait_send()
        block_copy(1, o).wait_send()
        block_pass(o).wait_send()
    for slot in (mine, 1, 0):
        each_side(lambda side: edge_copy(side, slot).wait_send())
    each_side(lambda side: edge_pass(side).wait_send())


def per_device(n_band, n_slab, orbitals, occupation):
    orbs, planes, cells = orbitals.shape
    tiles = cells // LANES
    ext = -(-(planes + 2 * WIDTH) // 8) * 8
    occ = jnp.broadcast_to(occupation[:, None, None], (orbs, planes, LANES))
    f32, bf16 = jnp.float32, jnp.bfloat16
    rows = 2 * orbs * WIDTH
    return pl.pallas_call(
        functools.partial(kernel, n_band, n_slab),
        out_shape=jax.ShapeDtypeStruct(orbitals.shape, f32),
        in_specs=[pl.BlockSpec(memory_space=pl.ANY)] * 2,
        out_specs=pl.BlockSpec(memory_space=pltpu.VMEM),
        scratch_shapes=[
            pltpu.VMEM((STEPS + 1, orbs, planes, cells + LANES), bf16),
            pltpu.VMEM((2, tiles // 2, rows, LANES), bf16),
            pltpu.VMEM((STEPS + 1, 2, tiles // 2, rows, LANES), bf16),
            pltpu.VMEM((orbs, tiles, ext, LANES), f32),
            pltpu.VMEM((orbs, 3, tiles, ext, LANES), f32),
            pltpu.VMEM((tiles, ext, LANES), f32),
            pltpu.VMEM((tiles, planes, LANES), f32),
            pltpu.VMEM((orbs, tiles, ext + 16, LANES), f32),
            pltpu.VMEM((orbs, tiles + 2, ext, LANES), f32),
            pltpu.VMEM((orbs, tiles, ext, LANES), f32),
            pltpu.VMEM((orbs, tiles + 2, ext, LANES), f32),
            pltpu.SemaphoreType.DMA((2,)),
            pltpu.SemaphoreType.DMA((STEPS, orbs)),
            pltpu.SemaphoreType.DMA((STEPS, orbs)),
            pltpu.SemaphoreType.DMA((STEPS + 1, 2)),
            pltpu.SemaphoreType.DMA((STEPS + 1, 2)),
        ],
        compiler_params=pltpu.CompilerParams(collective_id=0, has_side_effects=True),
        name="exchange",
    )(orbitals, occ)


def solution(mesh):
    in_specs = (P("band", "slab", None), P("band"))
    out_specs = P("band", "slab", None)
    return jax.shard_map(
        functools.partial(per_device, mesh.shape["band"], mesh.shape["slab"]),
        mesh=mesh, in_specs=in_specs, out_specs=out_specs, check_vma=False,
    )
```

time: 32.8 us -> 31.9 us (0.973)
  the two profiles are of different devices: /device:TPU:1 before, /device:TPU:0 now
where the time goes in v2:
time: 31.9 us; the launch traced here: 31.8 us
  Pallas kernels  28.6 us (90%)
  local copies, waits for them, and re-layouts  3.19 us (10%)
    pallas_call x1, Pallas kernels, per_device(): pl.pallas_call(functools.partial(kernel, n_band, n_slab), out_shape=jax.S...  28.6 us
    unnamed x1, local copies, waits for them, and re-layouts  1.87 us
    broadcast_in_dim x1, local copies, waits for them, and re-layouts, per_device(): occ = jnp.broadcast_to(occupation[:, None, None], (orbs, planes, LANES))  1.32 us

profile of v2, /device:TPU:0, one launch (start us, length us, event | category | flops | bytes accessed | tf_op | source)
XLA Modules:
  0.0 31.8 jit_solution(13192877754018559323)
XLA Ops:
  0.0 1.3 %broadcast_in_dim.2.occ_ref = bf16[2,16,128]{2,1,0:T(8,128)(2,1)} broadcast(bf16[2]{0:T(256)(128)(2,1)} %param.3), dimensions={0} | broadcast | bytes 8196 | tf_op jit(solution)/shard_map/broadcast_in_dim | solution.py:262
  1.3 28.6 %exchange.1 = f32[2,16,4096]{2,1,0:T(8,128)} custom-call(bf16[2,16,4096]{2,1,0:T(8,128)(2,1)} %orb_ref.1, bf16[2,16,128]{2,1,0:T(8,128)(2,1)} %broadcast_in_dim.2.occ_ref), custom_call_target="tpu_custom_call" | custom-call | tf_op jit(solution)/shard_map/exchange/pallas_call | solution.py:265
  29.9 1.9 %copy.4 = f32[2,16,4096]{2,1,0:T(8,128)} copy(f32[2,16,4096]{2,1,0:T(8,128)} %exchange.1) | data formatting | bytes 1048576

commit v3 on v2

--- a/solution.py
+++ b/solution.py
@@ -12,7 +12,7 @@
 STEPS = 3
 LANES = 128
 WIDTH = 2
-UNROLL = 4
+UNROLL = 8
 MESH = pl.DeviceIdType.MESH
 
 
@@ -56,9 +56,7 @@
     source = {mine: 0, 1: -2, 0: 2 * odd - 3}
 
     load = pltpu.make_async_copy(orb_ref, slots.at[mine, :, :, :cells], load_sem.at[0])
-    load_occ = pltpu.make_async_copy(occ_ref, slots.at[mine, :, :, cells:], load_sem.at[1])
     load.start()
-    load_occ.start()
 
     barrier = pltpu.get_barrier_semaphore()
     for by in (source[1], source[0]):
@@ -71,7 +69,9 @@
                 pl.semaphore_signal(barrier, inc=1, device_id=at(source[slot], step_of[side]), device_id_type=MESH)
 
     load.wait()
-    load_occ.wait()
+    for o in range(orbs):
+        value = jnp.broadcast_to(occ_ref[:, o:o + 1].astype(jnp.float32), (planes, LANES))
+        slots[mine, o, :, cells:] = value.astype(jnp.bfloat16)
 
     def cut(k):
         parts = ([], [])
@@ -152,20 +152,24 @@
     def from_right(mid):
         return pltpu.roll(jnp.where(first_col, 0.0, mid), LANES - 1, 1)
 
+    def pick(rows, h, o):
+        value = None
+        for q in range(orbs):
+            r = (h * orbs + q) * WIDTH
+            piece = rows[r:r + WIDTH]
+            value = piece if value is None else jnp.where(o == q, piece, value)
+        return value
+
     def widen(slot, o, dst):
         def body(k):
             low = halos[slot, 0, k].astype(jnp.float32)
             up = halos[slot, 1, k].astype(jnp.float32)
             for h in range(2):
                 t = 2 * k + h
-                for q in range(orbs):
-                    @pl.when(o == q)
-                    def _(q=q, h=h, t=t):
-                        r = (h * orbs + q) * WIDTH
-                        dst[t, :WIDTH] = low[r:r + WIDTH]
-                        dst[t, planes + WIDTH:planes + 2 * WIDTH] = up[r:r + WIDTH]
+                dst[t, :WIDTH] = pick(low, h, o)
+                dst[t, planes + WIDTH:planes + 2 * WIDTH] = pick(up, h, o)
                 dst[t, WIDTH:planes + WIDTH] = slots[slot, o, :, lane_tile(t)].astype(jnp.float32)
-        loop(tiles // 2, body, 2)
+        loop(tiles // 2, body, 4)
 
     def visit(slot, o):
         weight = -scale * slots[slot, o, :, cells:].astype(jnp.float32)
@@ -259,13 +263,13 @@
     orbs, planes, cells = orbitals.shape
     tiles = cells // LANES
     ext = -(-(planes + 2 * WIDTH) // 8) * 8
-    occ = jnp.broadcast_to(occupation[:, None, None], (orbs, planes, LANES))
+    occ = occupation.reshape(1, orbs)
     f32, bf16 = jnp.float32, jnp.bfloat16
     rows = 2 * orbs * WIDTH
     return pl.pallas_call(
         functools.partial(kernel, n_band, n_slab),
         out_shape=jax.ShapeDtypeStruct(orbitals.shape, f32),
-        in_specs=[pl.BlockSpec(memory_space=pl.ANY)] * 2,
+        in_specs=[pl.BlockSpec(memory_space=pl.ANY), pl.BlockSpec(memory_space=pltpu.VMEM)],
         out_specs=pl.BlockSpec(memory_space=pltpu.VMEM),
         scratch_shapes=[
             pltpu.VMEM((STEPS + 1, orbs, planes, cells + LANES), bf16),
@@ -279,7 +283,7 @@
             pltpu.VMEM((orbs, tiles + 2, ext, LANES), f32),
             pltpu.VMEM((orbs, tiles, ext, LANES), f32),
             pltpu.VMEM((orbs, tiles + 2, ext, LANES), f32),
-            pltpu.SemaphoreType.DMA((2,)),
+            pltpu.SemaphoreType.DMA((1,)),
             pltpu.SemaphoreType.DMA((STEPS, orbs)),
             pltpu.SemaphoreType.DMA((STEPS, orbs)),
             pltpu.SemaphoreType.DMA((STEPS + 1, 2)),

time: 31.9 us -> 26.4 us (0.83)
  Pallas kernels: 28.6 us -> 24.3 us
  local copies, waits for them, and re-layouts: 3.19 us -> 1.87 us
    pallas_call x1, Pallas kernels: 28.6 us -> 24.3 us  [per_device(): pl.pallas_call(functools.partial(kernel, n_band, n_slab), out_shape=jax.S...]
    broadcast_in_dim x1 -> x0, local copies, waits for them, and re-layouts: 1.32 us -> none  [per_device(): occ = jnp.broadcast_to(occupation[:, None, None], (orbs, planes, LANES))]
where the time goes in v3:
time: 26.4 us; the launch traced here: 26.2 us
  Pallas kernels  24.3 us (92%)
  local copies, waits for them, and re-layouts  1.87 us (7%)
    pallas_call x1, Pallas kernels, per_device(): pl.pallas_call(functools.partial(kernel, n_band, n_slab), out_shape=jax.S...  24.3 us
    unnamed x1, local copies, waits for them, and re-layouts  1.87 us

profile of v3, /device:TPU:0, one launch (start us, length us, event | category | flops | bytes accessed | tf_op | source)
XLA Modules:
  0.0 26.2 jit_solution(4555690903893815571)
XLA Ops:
  0.0 24.3 %exchange.1 = f32[2,16,4096]{2,1,0:T(8,128)} custom-call(bf16[2,16,4096]{2,1,0:T(8,128)(2,1)} %orb_ref.1, bf16[1,2]{1,0:T(2,128)(2,1)} %bitcast.1), custom_call_target="tpu_custom_call" | custom-call | tf_op jit(solution)/shard_map/exchange/pallas_call | solution.py:269
  24.4 1.9 %copy.4 = f32[2,16,4096]{2,1,0:T(8,128)} copy(f32[2,16,4096]{2,1,0:T(8,128)} %exchange.1) | data formatting | bytes 1048576

commit v4 on v3

--- a/solution.py
+++ b/solution.py
@@ -38,7 +38,7 @@
 
 
 def kernel(n_band, n_slab, orb_ref, occ_ref, out_ref, slots, edges, halos, own, own_moved, vis,
-           weighted, dens, turned, part, inner_field, load_sem, send_sem, recv_sem, edge_send, edge_recv):
+           weighted, dens, turned, part, inner_field, shifts, across, load_sem, send_sem, recv_sem, edge_send, edge_recv):
     orbs, planes, cells = orb_ref.shape
     tiles = cells // LANES
     ext = vis.shape[1]
@@ -137,20 +137,27 @@
             turned[i, t] = jnp.zeros(turned.shape[2:], jnp.float32)
             inner_field[i, t] = jnp.zeros(inner_field.shape[2:], jnp.float32)
 
-    lane = lax.broadcasted_iota(jnp.int32, (1, LANES), 1)
-    high = lane >= NZ
-    column = lane % NZ
-    first_col, last_col = column == 0, column == NZ - 1
+    high = lax.broadcasted_iota(jnp.int32, (1, LANES), 1) >= NZ
     row = lax.broadcasted_iota(jnp.int32, (ext, LANES), 0)
     below = jnp.where(has[0], 1.0, 0.0)
     above = jnp.where(has[1], 1.0, 0.0)
     row_mask = jnp.where(row == WIDTH - 1, below, jnp.where(row == planes + WIDTH, above, 1.0))
 
-    def from_left(mid):
-        return pltpu.roll(jnp.where(last_col, 0.0, mid), 1, 1)
-
-    def from_right(mid):
-        return pltpu.roll(jnp.where(first_col, 0.0, mid), LANES - 1, 1)
+    def ones(cond):
+        return jnp.where(cond, 1.0, 0.0)
+
+    src = lax.broadcasted_iota(jnp.int32, (LANES, LANES), 0)
+    dst_lane = lax.broadcasted_iota(jnp.int32, (LANES, LANES), 1)
+    swap = ones(src == (dst_lane + NZ) % LANES)
+    left = jnp.where(dst_lane % NZ == 0, 0.0, ones(src == dst_lane - 1))
+    right = jnp.where(dst_lane % NZ == NZ - 1, 0.0, ones(src == dst_lane + 1))
+    for n, matrix in enumerate((swap, left, right)):
+        shifts[:, n * LANES:(n + 1) * LANES] = matrix.astype(jnp.bfloat16)
+    across[:LANES] = (swap + left + right).astype(jnp.bfloat16)
+    across[LANES:] = swap.astype(jnp.bfloat16)
+
+    def moves(tile_rows):
+        return jnp.dot(tile_rows.astype(jnp.bfloat16), shifts[...], preferred_element_type=jnp.float32)
 
     def pick(rows, h, o):
         value = None
@@ -175,16 +182,21 @@
         weight = -scale * slots[slot, o, :, cells:].astype(jnp.float32)
         widen(slot, o, vis)
 
-        def density(t):
-            mid = vis[t]
-            moved = (pltpu.roll(mid, NZ, 1), from_left(mid), from_right(mid))
-            weighted[t] = weight * vis[t, WIDTH:planes + WIDTH]
-            for i in range(orbs):
-                d = own[i, t] * mid
-                dens[i, t, 8:ext + 8] = d
-                turn = own_moved[i, 0, t] * moved[0]
-                turned[i, t + 1] = turn
-                part[i, t] = inner * d + turn + (own_moved[i, 1, t] * moved[1] + own_moved[i, 2, t] * moved[2])
+        def density(k):
+            both = jnp.concatenate([vis[2 * k], vis[2 * k + 1]], axis=0)
+            moved = moves(both)
+            for h in range(2):
+                t = 2 * k + h
+                mid = both[h * ext:(h + 1) * ext]
+                turn_v, left_v, right_v = [
+                    moved[h * ext:(h + 1) * ext, n * LANES:(n + 1) * LANES] for n in range(3)]
+                weighted[t] = weight * vis[t, WIDTH:planes + WIDTH]
+                for i in range(orbs):
+                    d = own[i, t] * mid
+                    dens[i, t, 8:ext + 8] = d
+                    turn = own_moved[i, 0, t] * turn_v
+                    turned[i, t + 1] = turn
+                    part[i, t] = inner * d + turn + (own_moved[i, 1, t] * left_v + own_moved[i, 2, t] * right_v)
 
         def once(t):
             for i in range(orbs):
@@ -193,17 +205,24 @@
                 inner_field[i, t + 1] = u * row_mask
 
         def twice(t):
+            rows = slice(WIDTH, planes + WIDTH)
+            field = jnp.concatenate([
+                jnp.concatenate([inner_field[i, t + 1, rows] for i in range(orbs)], axis=0),
+                jnp.concatenate([
+                    jnp.where(high, inner_field[i, t, rows], inner_field[i, t + 2, rows])
+                    for i in range(orbs)], axis=0)], axis=1)
+            top = field.astype(jnp.bfloat16)
+            rest = (field - top.astype(jnp.float32)).astype(jnp.bfloat16)
+            matrix = across[...]
+            plane_sum = jnp.dot(top, matrix, preferred_element_type=jnp.float32)
+            plane_sum = plane_sum + jnp.dot(rest, matrix, preferred_element_type=jnp.float32)
             for i in range(orbs):
-                mid = inner_field[i, t + 1, WIDTH:planes + WIDTH]
-                before = inner_field[i, t, WIDTH:planes + WIDTH]
-                after = inner_field[i, t + 2, WIDTH:planes + WIDTH]
                 v = inner_field[i, t + 1, WIDTH - 1:planes + WIDTH - 1] + inner_field[i, t + 1, WIDTH + 1:planes + WIDTH + 1]
-                v = v + pltpu.roll(mid + jnp.where(high, before, after), NZ, 1)
-                v = v + (from_left(mid) + from_right(mid))
+                v = v + plane_sum[i * planes:(i + 1) * planes]
                 v = v + outer * dens[i, t, 8 + WIDTH:8 + planes + WIDTH]
                 out_ref[i, :, lane_tile(t)] += weighted[t] * v
 
-        loop(tiles, density, UNROLL)
+        loop(tiles // 2, density, UNROLL // 2)
         loop(tiles, once, UNROLL)
         loop(tiles, twice, UNROLL)
 
@@ -213,10 +232,9 @@
 
     def prepare(t):
         for i in range(orbs):
-            mid = own[i, t]
-            own_moved[i, 0, t] = pltpu.roll(mid, NZ, 1)
-            own_moved[i, 1, t] = from_left(mid)
-            own_moved[i, 2, t] = from_right(mid)
+            moved = moves(own[i, t])
+            for n in range(3):
+                own_moved[i, n, t] = moved[:, n * LANES:(n + 1) * LANES]
             out_ref[i, :, lane_tile(t)] = jnp.zeros((planes, LANES), jnp.float32)
 
     loop(tiles, prepare, UNROLL)
@@ -283,6 +301,8 @@
             pltpu.VMEM((orbs, tiles + 2, ext, LANES), f32),
             pltpu.VMEM((orbs, tiles, ext, LANES), f32),
             pltpu.VMEM((orbs, tiles + 2, ext, LANES), f32),
+            pltpu.VMEM((LANES, 3 * LANES), bf16),
+            pltpu.VMEM((2 * LANES, LANES), bf16),
             pltpu.SemaphoreType.DMA((1,)),
             pltpu.SemaphoreType.DMA((STEPS, orbs)),
             pltpu.SemaphoreType.DMA((STEPS, orbs)),

time: 26.4 us -> 30.7 us (1.16)
  Pallas kernels: 24.3 us -> 28.6 us
    pallas_call x1, Pallas kernels: 24.3 us -> 28.6 us  [per_device(): pl.pallas_call(functools.partial(kernel, n_band, n_slab), out_shape=jax.S...]
where the time goes in v4:
time: 30.7 us; the launch traced here: 30.4 us
  Pallas kernels  28.6 us (93%)
  local copies, waits for them, and re-layouts  1.87 us (6%)
    pallas_call x1, Pallas kernels, per_device(): pl.pallas_call(functools.partial(kernel, n_band, n_slab), out_shape=jax.S...  28.6 us
    unnamed x1, local copies, waits for them, and re-layouts  1.87 us

profile of v4, /device:TPU:0, one launch (start us, length us, event | category | flops | bytes accessed | tf_op | source)
XLA Modules:
  0.0 30.4 jit_solution(17334178928638273436)
XLA Ops:
  0.0 28.6 %exchange.1 = f32[2,16,4096]{2,1,0:T(8,128)} custom-call(bf16[2,16,4096]{2,1,0:T(8,128)(2,1)} %orb_ref.1, bf16[1,2]{1,0:T(2,128)(2,1)} %bitcast.1), custom_call_target="tpu_custom_call" | custom-call | tf_op jit(solution)/shard_map/exchange/pallas_call | solution.py:287
  28.6 1.9 %copy.4 = f32[2,16,4096]{2,1,0:T(8,128)} copy(f32[2,16,4096]{2,1,0:T(8,128)} %exchange.1) | data formatting | bytes 1048576
